TPU v7x, 32 devices: a whole 2x2x4 slice. The times are simulated.
32 devices in a mesh: term: 4 (over y, x), sector: 8 (over z, core).
Axes of the slice: x: 2, y: 2, z: 4, core: 2. Of those that a mesh axis runs over, the one named last changes fastest.
Arguments:
- wavefunction: float32 [8, 512, 512], P('sector'), may hold values from -120 to 120
- precond: float32 [8, 512, 512], P('sector', 'term'), may hold values from 0.05 to 4
- left_ops: float32 [8, 16, 512, 512], P('sector', 'term'), may hold values from -0.5 to 4.5
- right_ops: float32 [8, 16, 512, 512], P('sector', 'term'), may hold values from -1 to 2
- out_sector: int32 [8, 16], P('sector', 'term'), may hold values from 0 to 7, as said below
- live_counts: int32 [8, 4], P('sector', 'term'), may hold values from 1 to 4, as said below
Outputs:
- first_image: float32 [8, 512, 512], P('sector', 'term')
- correction: float32 [8, 512, 512], P('sector', 'term')
- second_image: float32 [8, 512, 512], P('sector', 'term')
Inputs may be any that keep to these rules, and one draw needn't show every extreme that they name: Each term moves the charge by at most one sector: out_sector[s, j] differs from s by at most 1. `live_counts`: in every sector some device has all 4 slots live.
All inputs are finite; a program needn't handle non-finite values.
Results may differ from a plain program's by a relative error of at most 0.0003.
Values sent between devices are 32-bit elements; how exact they have to be, the bound alone decides.
A program may use at most 64 MiB of HBM per device.

v0:
```python
import jax
import jax.numpy as jnp
from jax import lax
from jax.sharding import PartitionSpec as P


def from_behind(block, axis, distance):
    devices = range(lax.axis_size(axis))
    route = [(i - distance, i) for i in devices if i - distance in devices]
    return lax.ppermute(block, axis, route)


def matmul(first_op, second_op):
    return jnp.dot(
        first_op, second_op, precision=lax.Precision.HIGHEST, preferred_element_type=jnp.float32
    )


def term_rows(vector, left_stack, right_stack, offsets, kept, row_count):
    width = vector.shape[1]
    totals = jnp.zeros((row_count, 3, width), jnp.float32)

    def add_slot(slot_id, running):
        left_rows = left_stack[slot_id]
        product = matmul(matmul(left_rows, vector), right_stack[slot_id])
        return running.at[:, offsets[slot_id]].add(product)

    totals = lax.fori_loop(jnp.zeros((), jnp.int32), kept, add_slot, totals)
    return totals.reshape(row_count, 3 * width)


def per_device(wavefunction, precond, left_ops, right_ops, out_sector, live_counts):
    term_count = lax.axis_size("term")
    width = wavefunction.shape[1]
    slab_rows = width // term_count
    first_own = lax.axis_index("term") * slab_rows
    sector_id = lax.axis_index("sector")
    center = wavefunction[0]
    left_stack = left_ops[0]
    right_stack = right_ops[0]
    offsets = out_sector[0] - sector_id + 1
    count_here = live_counts[0, 0]

    def apply_hamiltonian(vector):
        whole = term_rows(vector, left_stack, right_stack, offsets, count_here, width).reshape(
            width, 3, width
        )
        upward = from_behind(whole[:, 2], "sector", 1)
        downward = from_behind(whole[:, 0], "sector", -1)
        return lax.psum_scatter(
            whole[:, 1] + upward + downward, "term", scatter_dimension=0, tiled=True
        )

    first_image = apply_hamiltonian(center)
    own_rows = lax.dynamic_slice_in_dim(center, first_own, slab_rows, 0)
    scaling = precond[0]
    cross, norm_sq = lax.psum(
        (jnp.sum(own_rows * first_image), jnp.sum(own_rows * own_rows)), ("term", "sector")
    )
    rayleigh = cross / norm_sq
    raw = scaling * (first_image - rayleigh * own_rows)
    correlation_sum = lax.psum(jnp.sum(own_rows * raw), ("term", "sector"))
    correction = raw - correlation_sum / norm_sq * own_rows
    full_correction = lax.all_gather(correction, "term", axis=0, tiled=True)
    second_image = apply_hamiltonian(full_correction)
    return (first_image[None], correction[None], second_image[None])


def solution(mesh):
    placed = (
        P("sector", None, None),
        P("sector", "term", None),
        P("sector", "term", None, None),
        P("sector", "term", None, None),
        P("sector", "term"),
        P("sector", "term"),
    )
    return jax.shard_map(
        per_device,
        mesh=mesh,
        in_specs=placed,
        out_specs=(P("sector", "term", None), P("sector", "term", None), P("sector", "term", None)),
        check_vma=False,
    )
```

profile of v0, /device:TPU:11, one launch (start us, length us, event | category | flops | bytes accessed | tf_op | source)
XLA Modules:
  0.0 316.4 jit_solution(16993770695380085301)
XLA Ops:
  8.3 11.7 %while.22 = (s32[]{:T(128)}, f32[512,3,512]{2,0,1:T(8,128)S(1)}, s32[]{:T(128)}, s32[4]{0:T(128)S(1)}, f32[4,512,512]{2,1,0:T(8,128)}, /*index=5*/f32[512,512]{1...) while((s32[]{:T(128)}, f32[512,3,512]{2,0,1:T(8,128)S(1)}, ...), condition=%wide.region_2.0_spmd, body=%wide.region_0.0_spmd.sunk | while | flops 3221749760 | bytes 7341298 | solution.py:28
  12.2 3.4 %fusion.44 = f32[512,512]{1,0:T(8,128)S(1)} fusion(f32[512,512]{1,0:T(8,128)} %get-tuple-element.260, f32[4,512,512]{2,1,0:T(8,128)} %get-tuple-element.259, s32[]{:T(128)S(6)} %select_n.28), kind=kOutput, calls=%fused_computation.4.clone.1 | convolution fusion | flops 1610612736 | bytes 3145732 | tf_op jit(solution)/shard_map/while/body/dot_general | solution.py:14
  15.6 3.8 %fusion.45 = f32[512,3,512]{2,0,1:T(8,128)S(1)} fusion(f32[512,3,512]{2,0,1:T(8,128)S(1)} %get-tuple-element.243, s32[]{:T(128)} %select_n.29, f32[512,512]{1,0:T(8,128)S(1)} %fusion.44, f32[4,512,512]{2,1,0:T(8,128)} %get-tuple-element.261, s32[]{:T(128)S(6)} %select_n.28, pred[]{:T(512)} %and_reduce_fusion.4), kind=kOutput, calls=%fused_computation.2.clone.1 | convolution fusion | flops 1611137024 | bytes 4195332 | tf_op jit(solution)/shard_map/while/body/dot_general | solution.py:14
  20.2 3.9 %collective-permute-start = (f32[512,512]{1,0:T(8,128)S(1)}, f32[512,512]{1,0:T(8,128)S(1)}, u32[]{:S(2)}, u32[]{:S(2)}) collective-permute-start(f32[512,512]{1,0:T(8,128)S(1)} %get-tuple-element.139), channel_id=1, source_target_pairs={{0,1},{1,2},{2,3},{3,4},{4,5},{5,6},{6,7},{8,9},{9,10},{10,11},{11... | collective-permute-start | bytes 3145736 | tf_op jit(solution)/shard_map/ppermute | solution.py:10
  24.1 1.9 collective-permute-start.1
  26.1 9.8 %collective-permute-done = f32[512,512]{1,0:T(8,128)S(1)} collective-permute-done((f32[512,512]{1,0:T(8,128)S(1)}, f32[512,512]{1,0:T(8,128)S(1)}, u32[]{:S(2)}, u32[]{:S(2)}) %collective-permute-start) | collective-permute-done | bytes 1048608 | tf_op jit(solution)/shard_map/ppermute | solution.py:10
  35.9 4.4 %collective-permute-done.1 = f32[512,512]{1,0:T(8,128)S(1)} collective-permute-done((f32[512,512]{1,0:T(8,128)S(1)}, f32[512,512]{1,0:T(8,128)S(1)}, u32[]{:S(2)}, u32[]{:S(2)}) %collective-permute-start.1) | collective-permute-done | bytes 1048608 | tf_op jit(solution)/shard_map/ppermute | solution.py:10
  40.2 1.4 fusion.17
  41.7 60.7 %reduce-scatter.3.cloned.1.call-done = f32[128,512]{1,0:T(8,128)} async-done(((f32[512,512]{1,0:T(8,128)}), f32[128,512]{1,0:T(8,128)}) %reduce-scatter.3.cloned.1.call-update) | async-done | bytes 262160 | tf_op jit(solution)/shard_map/reduce_scatter | solution.py:50
  102.4 1.7 fusion.19
  104.1 39.9 %all-reduce = (f32[]{:T(128)}, f32[]{:T(128)}) all-reduce(f32[]{:T(128)} %get-tuple-element.106, f32[]{:T(128)} %get-tuple-element.105), channel_id=1, replica_groups=mesh['term'=4,'sector'=8] {'term','sector'}, use_global_device_ids=true, to_apply=%region_5.0 | all-reduce | flops 2 | bytes 16 | tf_op jit(solution)/shard_map/psum | solution.py:57
  145.4 1.7 fusion.22
  147.1 39.5 %psum.23 = f32[]{:T(128)} all-reduce(f32[]{:T(128)} %fusion.22), channel_id=1, replica_groups=mesh['term'=4,'sector'=8] {'term','sector'}, use_global_device_ids=true, to_apply=%region_9.0 | all-reduce | flops 1 | bytes 8 | tf_op jit(solution)/shard_map/psum | solution.py:62
  187.9 1.8 fusion.23
  189.8 28.0 %all-gather.2.cloned.1.call-done = f32[512,512]{1,0:T(8,128)} async-done(((f32[128,512]{1,0:T(8,128)}), f32[512,512]{1,0:T(8,128)}) %all-gather.2.cloned.1.call-update) | async-done | bytes 1048592 | tf_op jit(solution)/shard_map/all_gather | solution.py:64
  218.2 11.4 %while.23 = (s32[]{:T(128)}, f32[512,3,512]{2,0,1:T(8,128)S(1)}, s32[]{:T(128)}, s32[4]{0:T(128)S(1)}, f32[4,512,512]{2,1,0:T(8,128)}, /*index=5*/f32[512,512]{1...) while((s32[]{:T(128)}, f32[512,3,512]{2,0,1:T(8,128)S(1)}, ...), condition=%wide.region_12.0_spmd, body=%wide.region_10.0_spmd.sunk | while | flops 3221749760 | bytes 7341298 | solution.py:28
  221.8 3.4 %fusion.50 = f32[512,512]{1,0:T(8,128)S(1)} fusion(f32[512,512]{1,0:T(8,128)} %get-tuple-element.299, f32[4,512,512]{2,1,0:T(8,128)} %get-tuple-element.298, s32[]{:T(128)S(6)} %select_n.30), kind=kOutput, calls=%fused_computation.15.clone.1 | convolution fusion | flops 1610612736 | bytes 3145732 | tf_op jit(solution)/shard_map/while/body/dot_general | solution.py:14
  225.2 3.7 %fusion.51 = f32[512,3,512]{2,0,1:T(8,128)S(1)} fusion(f32[512,3,512]{2,0,1:T(8,128)S(1)} %get-tuple-element.282, s32[]{:T(128)} %select_n.31, f32[512,512]{1,0:T(8,128)S(1)} %fusion.50, f32[4,512,512]{2,1,0:T(8,128)} %get-tuple-element.300, s32[]{:T(128)S(6)} %select_n.30, pred[]{:T(512)} %and_reduce_fusion.5), kind=kOutput, calls=%fused_computation.13.clone.1 | convolution fusion | flops 1611137024 | bytes 4195332 | tf_op jit(solution)/shard_map/while/body/dot_general | solution.py:14
  229.8 3.8 %collective-permute-start.2 = (f32[512,512]{1,0:T(8,128)S(1)}, f32[512,512]{1,0:T(8,128)S(1)}, u32[]{:S(2)}, u32[]{:S(2)}) collective-permute-start(f32[512,512]{1,0:T(8,128)S(1)} %get-tuple-element.137), channel_id=1, source_target_pairs={{0,1},{1,2},{2,3},{3,4},{4,5},{5,6},{6,7},{8,9},{9,10},{10,11},{11... | collective-permute-start | bytes 3145736 | tf_op jit(solution)/shard_map/ppermute | solution.py:10
  233.6 1.9 collective-permute-start.3
  235.5 9.8 %collective-permute-done.2 = f32[512,512]{1,0:T(8,128)S(1)} collective-permute-done((f32[512,512]{1,0:T(8,128)S(1)}, f32[512,512]{1,0:T(8,128)S(1)}, u32[]{:S(2)}, u32[]{:S(2)}) %collective-permute-start.2) | collective-permute-done | bytes 1048608 | tf_op jit(solution)/shard_map/ppermute | solution.py:10
  245.3 4.4 %collective-permute-done.3 = f32[512,512]{1,0:T(8,128)S(1)} collective-permute-done((f32[512,512]{1,0:T(8,128)S(1)}, f32[512,512]{1,0:T(8,128)S(1)}, u32[]{:S(2)}, u32[]{:S(2)}) %collective-permute-start.3) | collective-permute-done | bytes 1048608 | tf_op jit(solution)/shard_map/ppermute | solution.py:10
  249.7 1.4 fusion.16
  251.1 58.7 %reduce-scatter.5.cloned.1.call-done = f32[128,512]{1,0:T(8,128)} async-done(((f32[512,512]{1,0:T(8,128)}), f32[128,512]{1,0:T(8,128)}) %reduce-scatter.5.cloned.1.call-update) | async-done | bytes 262160 | tf_op jit(solution)/shard_map/reduce_scatter | solution.py:50
  (19 shorter events, 4.5 us)
Async XLA Ops:
  7.2 1.1 copy-start.1
  7.2 95.2 %reduce-scatter.3.cloned.1.call-start = ((), (), s32[]{:S(2)}) async-start(), calls=%async_computation.2 | async-start | bytes 1310720 | tf_op jit(solution)/shard_map/reduce_scatter | solution.py:50
  20.2 125.2 %copy-start = (f32[1,128,512]{2,1,0:T(8,128)S(1)}, f32[1,128,512]{2,1,0:T(8,128)}, u32[]{:S(2)}) copy-start(f32[1,128,512]{2,1,0:T(8,128)} %param.15) | copy-start | bytes 786436
  20.2 15.6 %collective-permute-start = (f32[512,512]{1,0:T(8,128)S(1)}, f32[512,512]{1,0:T(8,128)S(1)}, u32[]{:S(2)}, u32[]{:S(2)}) collective-permute-start(f32[512,512]{1,0:T(8,128)S(1)} %get-tuple-element.139), channel_id=1, source_target_pairs={{0,1},{1,2},{2,3},{3,4},{4,5},{5,6},{6,7},{8,9},{9,10},{10,11},{11... | collective-permute-start | bytes 3145736 | tf_op jit(solution)/shard_map/ppermute | solution.py:10
  24.1 16.1 %collective-permute-start.1 = (f32[512,512]{1,0:T(8,128)S(1)}, f32[512,512]{1,0:T(8,128)S(1)}, u32[]{:S(2)}, u32[]{:S(2)}) collective-permute-start(f32[512,512]{1,0:T(8,128)S(1)} %get-tuple-element.140), channel_id=1, source_target_pairs={{1,0},{2,1},{3,2},{4,3},{5,4},{6,5},{7,6},{9,8},{10,9},{11,10},{12... | collective-permute-start | bytes 3145736 | tf_op jit(solution)/shard_map/ppermute | solution.py:10
  41.6 176.2 %all-gather.2.cloned.1.call-start = ((), (), s32[]{:S(2)}) async-start(), calls=%async_computation.3 | async-start | bytes 1310720 | tf_op jit(solution)/shard_map/all_gather | solution.py:64
  189.7 120.1 %reduce-scatter.5.cloned.1.call-start = ((), (), s32[]{:S(2)}) async-start(), calls=%async_computation.4 | async-start | bytes 1310720 | tf_op jit(solution)/shard_map/reduce_scatter | solution.py:50
  229.8 15.6 %collective-permute-start.2 = (f32[512,512]{1,0:T(8,128)S(1)}, f32[512,512]{1,0:T(8,128)S(1)}, u32[]{:S(2)}, u32[]{:S(2)}) collective-permute-start(f32[512,512]{1,0:T(8,128)S(1)} %get-tuple-element.137), channel_id=1, source_target_pairs={{0,1},{1,2},{2,3},{3,4},{4,5},{5,6},{6,7},{8,9},{9,10},{10,11},{11... | collective-permute-start | bytes 3145736 | tf_op jit(solution)/shard_map/ppermute | solution.py:10
  233.6 16.1 %collective-permute-start.3 = (f32[512,512]{1,0:T(8,128)S(1)}, f32[512,512]{1,0:T(8,128)S(1)}, u32[]{:S(2)}, u32[]{:S(2)}) collective-permute-start(f32[512,512]{1,0:T(8,128)S(1)} %get-tuple-element.138), channel_id=1, source_target_pairs={{1,0},{2,1},{3,2},{4,3},{5,4},{6,5},{7,6},{9,8},{10,9},{11,10},{12... | collective-permute-start | bytes 3145736 | tf_op jit(solution)/shard_map/ppermute | solution.py:10
Sparse Core Ops, SparseCore 0:
  41.8 60.6 reduce-scatter.2
  189.9 27.8 all-gather.1
  251.2 58.5 reduce-scatter.4
where the time goes:
time: 319 us; the launch traced here: 316 us
  waiting for transfers between devices  176 us (55%)
  blocking collectives  79.4 us (25%)
  between operations  16.5 us (5%)
  matrix products  14.2 us (4%)
  starting transfers between devices  11.7 us (4%)
  other arithmetic  10 us (3%)
  loops' own time  6.29 us (2%)
    reduce_scatter x2, waiting for transfers between devices, apply_hamiltonian(): lax.psum_scatter(whole[:, 1] + upward + downward, 'term', scatter_dimensi...  119 us
    psum x1, blocking collectives, per_device(): lax.psum((jnp.sum(own_rows * first_image), jnp.sum(own_rows * own_rows)),...  39.9 us
    psum x1, blocking collectives, per_device(): correlation_sum = lax.psum(jnp.sum(own_rows * raw), ('term', 'sector'))  39.5 us
    ppermute x4, waiting for transfers between devices, from_behind(): return lax.ppermute(block, axis, route)  28.4 us
    all_gather x1, waiting for transfers between devices, per_device(): full_correction = lax.all_gather(correction, 'term', axis=0, tiled=True)  28 us
    dot_general x4, matrix products, matmul(): jnp.dot(first_op, second_op, precision=lax.Precision.HIGHEST, preferred_e...  14.2 us
    ppermute x4, starting transfers between devices, from_behind(): return lax.ppermute(block, axis, route)  11.6 us
  transfers between devices with their start and end apart: 7, of which 7 were waited for; matrix products, arithmetic and copies ran while one was open for 0% of the time, Pallas kernels for 0%

commit v1 on v0

v1 whole, which is shorter than its diff:
```python
import functools

import jax
import jax.numpy as jnp
from jax import lax
from jax.experimental import pallas as pl
from jax.experimental.pallas import tpu as pltpu
from jax.sharding import PartitionSpec as P

F32 = jnp.float32
MESH = pl.DeviceIdType.MESH
VMEM = pl.BlockSpec(memory_space=pltpu.VMEM)


def split(x):
    high = x.astype(jnp.bfloat16)
    return high, (x - high.astype(F32)).astype(jnp.bfloat16)


def product(a_high, a_low, b_high, b_low):
    dot = functools.partial(jnp.dot, preferred_element_type=F32)
    return dot(a_high, b_high) + dot(a_high, b_low) + dot(a_low, b_high)


def terms_kernel(target, count, v_ref, left_ref, right_ref, out_ref, v_high, v_low, r_high, r_low):
    slot = pl.program_id(0)
    width = v_ref.shape[0]
    piece = min(256, width)

    @pl.when(slot == 0)
    def _():
        out_ref[...] = jnp.zeros_like(out_ref)
        v_high[...], v_low[...] = split(v_ref[...])

    @pl.when(slot < count[0, 0])
    def _():
        place = target[0, slot] - lax.axis_index("sector") + 1
        r_high[...], r_low[...] = split(right_ref[...])
        for start in range(0, width, piece):
            rows = pl.ds(start, piece)
            left_high, left_low = split(left_ref[rows])
            inner = product(left_high, left_low, v_high[...], v_low[...])
            in_high, in_low = split(inner)
            out_ref[place, rows] += product(in_high, in_low, r_high[...], r_low[...])


def all_terms(vector, left_ops, right_ops, out_sector, live_counts):
    slots, width = left_ops.shape[1], left_ops.shape[2]

    def live(j, target, count):
        return (0, jnp.minimum(j, count[0, 0] - 1), 0, 0)

    return pl.pallas_call(
        terms_kernel,
        out_shape=jax.ShapeDtypeStruct((3, width, width), F32),
        grid_spec=pltpu.PrefetchScalarGridSpec(
            num_scalar_prefetch=2,
            grid=(slots,),
            in_specs=[
                pl.BlockSpec((width, width), lambda j, a, b: (0, 0)),
                pl.BlockSpec((None, None, width, width), live),
                pl.BlockSpec((None, None, width, width), live),
            ],
            out_specs=pl.BlockSpec((3, width, width), lambda j, a, b: (0, 0, 0)),
            scratch_shapes=[pltpu.VMEM((width, width), jnp.bfloat16)] * 4,
        ),
        compiler_params=pltpu.CompilerParams(dimension_semantics=("arbitrary",), vmem_limit_bytes=40 << 20),
    )(out_sector, live_counts, vector, left_ops, right_ops)


def send(source, target, send_sem, recv_sem, **where):
    return pltpu.make_async_remote_copy(
        src_ref=source, dst_ref=target, send_sem=send_sem, recv_sem=recv_sem,
        device_id=where, device_id_type=MESH,
    )


def greet():
    terms, sectors = lax.axis_size("term"), lax.axis_size("sector")
    t, s = lax.axis_index("term"), lax.axis_index("sector")
    barrier = pltpu.get_barrier_semaphore()
    for k in range(1, terms):
        pl.semaphore_signal(barrier, inc=1, device_id={"term": lax.rem(t + k, terms)}, device_id_type=MESH)
    for k in range(1, sectors):
        pl.semaphore_signal(barrier, inc=1, device_id={"sector": lax.rem(s + k, sectors)}, device_id_type=MESH)
    pl.semaphore_wait(barrier, terms + sectors - 2)


def exchange(whole, image, bufs):
    up_in, down_in, acc, rs_in, up_s, up_r, down_s, down_r, rs_s, rs_r = bufs
    terms, sectors = lax.axis_size("term"), lax.axis_size("sector")
    t, s = lax.axis_index("term"), lax.axis_index("sector")
    rows = whole.shape[1] // terms

    def slab(r):
        return pl.ds(pl.multiple_of(r * rows, rows), rows)

    def upward(r):
        return send(whole.at[2, slab(r)], up_in.at[slab(r)], up_s.at[r], up_r.at[r], sector=lax.rem(s + 1, sectors))

    def downward(r):
        return send(whole.at[0, slab(r)], down_in.at[slab(r)], down_s.at[r], down_r.at[r],
                    sector=lax.rem(s + sectors - 1, sectors))

    def scatter(r, source):
        return send(acc.at[slab(r)], rs_in.at[source], rs_s.at[r], rs_r.at[source], term=r)

    @pl.loop(0, terms)
    def _(k):
        r = lax.rem(t + 1 + k, terms)

        @pl.when(s + 1 < sectors)
        def _():
            upward(r).start()

        @pl.when(s > 0)
        def _():
            downward(r).start()

    @pl.loop(0, terms)
    def _(k):
        r = lax.rem(t + 1 + k, terms)
        acc[slab(r)] = whole[1, slab(r)]

        @pl.when(s > 0)
        def _():
            upward(r).wait_recv()
            acc[slab(r)] += up_in[slab(r)]

        @pl.when(s + 1 < sectors)
        def _():
            downward(r).wait_recv()
            acc[slab(r)] += down_in[slab(r)]

        @pl.when(k < terms - 1)
        def _():
            scatter(r, t).start()

    image[...] = acc[slab(t)]

    @pl.loop(0, terms - 1)
    def _(k):
        j = lax.rem(t + terms - 1 - k, terms)
        scatter(j, j).wait_recv()
        image[...] += rs_in[j]

    def finish():
        @pl.loop(0, terms)
        def _(k):
            r = lax.rem(t + 1 + k, terms)

            @pl.when(s + 1 < sectors)
            def _():
                upward(r).wait_send()

            @pl.when(s > 0)
            def _():
                downward(r).wait_send()

            @pl.when(k < terms - 1)
            def _():
                scatter(r, t).wait_send()

    return finish


def exchange_scratch(width, terms):
    rows = width // terms
    return [pltpu.VMEM((width, width), F32)] * 3 + [pltpu.VMEM((terms, rows, width), F32)] + [
        pltpu.SemaphoreType.DMA((terms,))
    ] * 6


def first_kernel(whole, wave, precond, image, correction, full, *scratch):
    bufs, (gather, own, mid, term_in, sector_in, ag_s, ag_r, ts_s, ts_r, ss_s, ss_r) = scratch[:10], scratch[10:]
    terms, sectors = lax.axis_size("term"), lax.axis_size("sector")
    t, s = lax.axis_index("term"), lax.axis_index("sector")
    rows = image.shape[0]
    greet()
    finish = exchange(whole, image, bufs)

    w = wave[pl.ds(pl.multiple_of(t * rows, rows), rows)]
    f = image[...]
    p = precond[...]
    wf, ww = w * f, w * w

    def lanes(x):
        line = jnp.sum(x, axis=0, keepdims=True)
        return sum(line[:, c : c + 128] for c in range(0, line.shape[1], 128))

    own[...] = jnp.zeros_like(own)
    for i, x in enumerate((wf, ww, wf * p, ww * p)):
        own[i : i + 1] = lanes(x)

    def to_term(k):
        return send(own, term_in.at[k - 1], ts_s.at[k - 1], ts_r.at[k - 1], term=lax.rem(t + k, terms))

    def to_sector(k):
        return send(mid, sector_in.at[k - 1], ss_s.at[k - 1], ss_r.at[k - 1], sector=lax.rem(s + k, sectors))

    for k in range(1, terms):
        to_term(k).start()
    total = own[...]
    for k in range(1, terms):
        to_term(k).wait_recv()
        total += term_in[k - 1]
    mid[...] = total
    for k in range(1, sectors):
        to_sector(k).start()
    for k in range(1, sectors):
        to_sector(k).wait_recv()
        total += sector_in[k - 1]
    cross, norm, a, b = (jnp.sum(total[i : i + 1], axis=1, keepdims=True) for i in range(4))
    rayleigh = cross / norm
    share = (a - rayleigh * b) / norm
    gather[t] = p * (f - rayleigh * w) - share * w

    def spread(r, source):
        return send(gather.at[source], gather.at[source], ag_s.at[r], ag_r.at[source], term=r)

    for k in range(1, terms):
        spread(lax.rem(t + k, terms), t).start()
    correction[...] = gather[t]
    full[pl.ds(pl.multiple_of(t * rows, rows), rows)] = gather[t]
    for k in range(1, terms):
        j = lax.rem(t + terms - k, terms)
        spread(j, j).wait_recv()
        full[pl.ds(pl.multiple_of(j * rows, rows), rows)] = gather[j]
    finish()
    for k in range(1, terms):
        spread(lax.rem(t + k, terms), t).wait_send()
        to_term(k).wait_send()
    for k in range(1, sectors):
        to_sector(k).wait_send()


def second_kernel(whole, image, *scratch):
    greet()
    exchange(whole, image, scratch)()


def per_device(wavefunction, precond, left_ops, right_ops, out_sector, live_counts):
    terms, sectors = lax.axis_size("term"), lax.axis_size("sector")
    width = wavefunction.shape[1]
    rows = width // terms
    center = wavefunction[0]
    slab = jax.ShapeDtypeStruct((rows, width), F32)
    whole = all_terms(center, left_ops, right_ops, out_sector, live_counts)
    tile = pltpu.VMEM((8, 128), F32)
    dma = pltpu.SemaphoreType.DMA
    first_image, correction, full = pl.pallas_call(
        first_kernel,
        out_shape=(slab, slab, jax.ShapeDtypeStruct((width, width), F32)),
        in_specs=[VMEM] * 3,
        out_specs=(VMEM,) * 3,
        scratch_shapes=exchange_scratch(width, terms) + [
            pltpu.VMEM((terms, rows, width), F32), tile, tile,
            pltpu.VMEM((terms - 1, 8, 128), F32), pltpu.VMEM((sectors - 1, 8, 128), F32),
            dma((terms,)), dma((terms,)), dma((terms - 1,)), dma((terms - 1,)),
            dma((sectors - 1,)), dma((sectors - 1,)),
        ],
        compiler_params=pltpu.CompilerParams(collective_id=0, has_side_effects=True, vmem_limit_bytes=32 << 20),
    )(whole, center, precond[0])
    whole = all_terms(full, left_ops, right_ops, out_sector, live_counts)
    second_image = pl.pallas_call(
        second_kernel,
        out_shape=slab,
        in_specs=[VMEM],
        out_specs=VMEM,
        scratch_shapes=exchange_scratch(width, terms),
        compiler_params=pltpu.CompilerParams(collective_id=1, has_side_effects=True, vmem_limit_bytes=32 << 20),
    )(whole)
    return (first_image[None], correction[None], second_image[None])


def solution(mesh):
    placed = (
        P("sector", None, None),
        P("sector", "term", None),
        P("sector", "term", None, None),
        P("sector", "term", None, None),
        P("sector", "term"),
        P("sector", "term"),
    )
    return jax.shard_map(
        per_device,
        mesh=mesh,
        in_specs=placed,
        out_specs=(P("sector", "term", None), P("sector", "term", None), P("sector", "term", None)),
        check_vma=False,
    )
```

time: 319 us -> 95.3 us (0.30)
  waiting for transfers between devices: 176 us -> 0 us
  Pallas kernels: 0 us -> 85.3 us
  blocking collectives: 79.4 us -> 0 us
  between operations: 16.5 us -> 1.36 us
  matrix products: 14.2 us -> 0 us
  starting transfers between devices: 11.7 us -> 0 us
  other arithmetic: 10 us -> 0 us
  loops' own time: 6.29 us -> 0 us
  local copies, waits for them, and re-layouts: 2.3 us -> 8.38 us
    reduce_scatter x2 -> x0, waiting for transfers between devices: 119 us -> none  [apply_hamiltonian(): lax.psum_scatter(whole[:, 1] + upward + downward, 'term', scatter_dimensi...]
    pallas_call x0 -> x4, Pallas kernels: none -> 85.3 us  [the longest x1 49.7 us: per_device(): pl.pallas_call(first_kernel, out_shape=(slab, slab, jax.ShapeDtypeStruct(...]
    psum x2 -> x0, blocking collectives: 79.4 us -> none  [the longest x1 39.9 us: per_device(): lax.psum((jnp.sum(own_rows * first_image), jnp.sum(own_rows * own_rows)),...]
    ppermute x4 -> x0, waiting for transfers between devices: 28.4 us -> none  [from_behind(): return lax.ppermute(block, axis, route)]
    all_gather x1 -> x0, waiting for transfers between devices: 28 us -> none  [per_device(): full_correction = lax.all_gather(correction, 'term', axis=0, tiled=True)]
    dot_general x4 -> x0, matrix products: 14.2 us -> none  [matmul(): jnp.dot(first_op, second_op, precision=lax.Precision.HIGHEST, preferred_e...]
    ppermute x4 -> x0, starting transfers between devices: 11.6 us -> none  [from_behind(): return lax.ppermute(block, axis, route)]
    unnamed x4 -> x19, local copies, waits for them, and re-layouts: 0.01 us -> 8.38 us
  transfers between devices with their start and end apart: 7 -> 0, of which waited for: 7 -> 0; matrix products, arithmetic and copies ran while one was open for 0% -> 0% of each run, Pallas kernels for 0% -> 0%
where the time goes in v1:
time: 95.3 us; the launch traced here: 95.1 us
  Pallas kernels  85.3 us (90%)
  local copies, waits for them, and re-layouts  8.38 us (9%)
  between operations  1.36 us (1%)
    pallas_call x1, Pallas kernels, per_device(): pl.pallas_call(first_kernel, out_shape=(slab, slab, jax.ShapeDtypeStruct(...  49.7 us
    pallas_call x1, Pallas kernels, per_device(): pl.pallas_call(second_kernel, out_shape=slab, in_specs=[VMEM], out_specs=...  29.6 us
    unnamed x19, local copies, waits for them, and re-layouts  8.38 us
    pallas_call x2, Pallas kernels, all_terms(): pl.pallas_call(terms_kernel, out_shape=jax.ShapeDtypeStruct((3, width, wi...  6.02 us

profile of v1, /device:TPU:11, one launch (start us, length us, event | category | flops | bytes accessed | tf_op | source)
XLA Modules:
  0.0 95.1 jit_solution(3985895696022689056)
XLA Ops:
  1.3 0.0 copy-start
  1.3 2.2 %copy-done = f32[1,4,512,512]{3,2,1,0:T(8,128)S(1)} copy-done((f32[1,4,512,512]{3,2,1,0:T(8,128)S(1)}, f32[1,4,512,512]{3,2,1,0:T(8,128)}, u32[]{:S(2)}) %copy-start) | copy-done | bytes 4194328
  3.5 0.0 copy-start.2
  3.5 2.2 %copy-done.2 = f32[1,4,512,512]{3,2,1,0:T(8,128)S(1)} copy-done((f32[1,4,512,512]{3,2,1,0:T(8,128)S(1)}, f32[1,4,512,512]{3,2,1,0:T(8,128)}, u32[]{:S(2)}) %copy-start.2) | copy-done | bytes 4194328
  5.7 0.0 copy-start.4
  5.7 1.2 %copy-done.4 = f32[1,512,512]{2,1,0:T(8,128)S(1)} copy-done((f32[1,512,512]{2,1,0:T(8,128)S(1)}, f32[1,512,512]{2,1,0:T(8,128)}, u32[]{:S(2)}) %copy-start.4) | copy-done | bytes 1048600
  6.9 0.0 copy-start.7
  6.9 0.7 copy-done.7
  7.5 0.0 copy-start.5
  7.5 0.0 copy-start.6
  7.5 0.0 copy-start.3
  7.5 3.0 %shard_map.85.whole = f32[3,512,512]{2,1,0:T(8,128)S(1)} custom-call(s32[1,4]{1,0:T(1,128)S(1)} %copy-done.7, s32[1,1]{1,0:T(1,128)S(6)} %copy.12.count, f32[512,512]{1,0:T(8,128)S(1)} %bitcast.5, f32[1,4,512,512]{3,2,1,0:T(8,128)S(1)} %copy-done, f32[1,4,512,512]{3,2,1,0:T(8,128)S(1)} %copy-done.2), custom_call_target="tpu_custom_call" | custom-call | tf_op jit(solution)/shard_map/pallas_call | solution.py:53
  10.6 0.0 copy-done.5
  10.6 0.0 copy-done.6
  10.6 0.0 copy-start.1
  10.6 49.7 %shard_map.86 = (f32[128,512]{1,0:T(8,128)S(1)}, f32[128,512]{1,0:T(8,128)S(1)}, f32[512,512]{1,0:T(8,128)S(1)}) custom-call(f32[3,512,512]{2,1,0:T(8,128)S(1)} %shard_map.85.whole, f32[512,512]{1,0:T(8,128)S(1)} %bitcast.6, f32[128,512]{1,0:T(8,128)S(1)} %bitcast.8), custom_call_target="tpu_custom_call" | custom-call | tf_op jit(solution)/shard_map/pallas_call | solution.py:251
  60.3 0.0 copy-done.3
  60.3 0.0 copy-done.1
  60.4 3.0 %shard_map.87.whole = f32[3,512,512]{2,1,0:T(8,128)S(1)} custom-call(s32[1,4]{1,0:T(1,128)S(1)} %copy-done.7, s32[1,1]{1,0:T(1,128)S(6)} %copy.12.count, f32[512,512]{1,0:T(8,128)S(1)} %get-tuple-element.8.v_ref, f32[1,4,512,512]{3,2,1,0:T(8,128)S(1)} %copy-done.1, f32[1,4,512,512]{3,2,1,0:T(8,128)S(1)} %copy-done.3), custom_call_target="tpu_custom_call" | custom-call | tf_op jit(solution)/shard_map/pallas_call | solution.py:53
  63.4 29.6 %shard_map.88 = f32[128,512]{1,0:T(8,128)S(1)} custom-call(f32[3,512,512]{2,1,0:T(8,128)S(1)} %shard_map.87.whole), custom_call_target="tpu_custom_call" | custom-call | tf_op jit(solution)/shard_map/pallas_call | solution.py:265
  93.0 0.7 copy.13
  93.7 0.7 copy.14
  94.4 0.7 copy.15
Async XLA Ops:
  1.3 2.2 %copy-start = (f32[1,4,512,512]{3,2,1,0:T(8,128)S(1)}, f32[1,4,512,512]{3,2,1,0:T(8,128)}, u32[]{:S(2)}) copy-start(f32[1,4,512,512]{3,2,1,0:T(8,128)} %left_ref.3) | copy-start | bytes 12582916
  3.5 2.2 %copy-start.2 = (f32[1,4,512,512]{3,2,1,0:T(8,128)S(1)}, f32[1,4,512,512]{3,2,1,0:T(8,128)}, u32[]{:S(2)}) copy-start(f32[1,4,512,512]{3,2,1,0:T(8,128)} %right_ref.3) | copy-start | bytes 12582916
  5.7 1.2 %copy-start.4 = (f32[1,512,512]{2,1,0:T(8,128)S(1)}, f32[1,512,512]{2,1,0:T(8,128)}, u32[]{:S(2)}) copy-start(f32[1,512,512]{2,1,0:T(8,128)} %param.6) | copy-start | bytes 3145732
  6.9 0.7 copy-start.7
  7.5 3.0 %copy-start.5 = (f32[1,512,512]{2,1,0:T(8,128)S(1)}, f32[1,512,512]{2,1,0:T(8,128)}, u32[]{:S(2)}) copy-start(f32[1,512,512]{2,1,0:T(8,128)} %param.6) | copy-start | bytes 3145732
  7.5 3.0 %copy-start.6 = (f32[1,128,512]{2,1,0:T(8,128)S(1)}, f32[1,128,512]{2,1,0:T(8,128)}, u32[]{:S(2)}) copy-start(f32[1,128,512]{2,1,0:T(8,128)} %param.7) | copy-start | bytes 786436
  7.5 52.8 %copy-start.3 = (f32[1,4,512,512]{3,2,1,0:T(8,128)S(1)}, f32[1,4,512,512]{3,2,1,0:T(8,128)}, u32[]{:S(2)}) copy-start(f32[1,4,512,512]{3,2,1,0:T(8,128)} %right_ref.3) | copy-start | bytes 12582916
  10.6 49.8 %copy-start.1 = (f32[1,4,512,512]{3,2,1,0:T(8,128)S(1)}, f32[1,4,512,512]{3,2,1,0:T(8,128)}, u32[]{:S(2)}) copy-start(f32[1,4,512,512]{3,2,1,0:T(8,128)} %left_ref.3) | copy-start | bytes 12582916

commit v2 on v1

--- a/solution.py
+++ b/solution.py
@@ -64,7 +64,7 @@
             out_specs=pl.BlockSpec((3, width, width), lambda j, a, b: (0, 0, 0)),
             scratch_shapes=[pltpu.VMEM((width, width), jnp.bfloat16)] * 4,
         ),
-        compiler_params=pltpu.CompilerParams(dimension_semantics=("arbitrary",), vmem_limit_bytes=40 << 20),
+        compiler_params=pltpu.CompilerParams(dimension_semantics=("arbitrary",), vmem_limit_bytes=58 << 20),
     )(out_sector, live_counts, vector, left_ops, right_ops)
 
 

time: 95.3 us -> 101 us (1.060); the launches traced: 95.1 us -> 99.6 us
  Pallas kernels: 85.3 us -> 91.5 us
  local copies, waits for them, and re-layouts: 8.38 us -> 6.86 us
    pallas_call x2, Pallas kernels: 6.02 us -> 13.3 us  [all_terms(): pl.pallas_call(terms_kernel, out_shape=jax.ShapeDtypeStruct((3, width, wi...]
    unnamed x19 -> x13, local copies, waits for them, and re-layouts: 8.38 us -> 6.86 us
    pallas_call x1, Pallas kernels: 29.6 us -> 28.3 us  [per_device(): pl.pallas_call(second_kernel, out_shape=slab, in_specs=[VMEM], out_specs=...]
where the time goes in v2:
time: 101 us; the launch traced here: 99.6 us
  Pallas kernels  91.5 us (91%)
  local copies, waits for them, and re-layouts  6.86 us (7%)
  between operations  1.33 us (1%)
    pallas_call x1, Pallas kernels, per_device(): pl.pallas_call(first_kernel, out_shape=(slab, slab, jax.ShapeDtypeStruct(...  49.8 us
    pallas_call x1, Pallas kernels, per_device(): pl.pallas_call(second_kernel, out_shape=slab, in_specs=[VMEM], out_specs=...  28.3 us
    pallas_call x2, Pallas kernels, all_terms(): pl.pallas_call(terms_kernel, out_shape=jax.ShapeDtypeStruct((3, width, wi...  13.3 us
    unnamed x13, local copies, waits for them, and re-layouts  6.86 us

profile of v2, /device:TPU:11, one launch (start us, length us, event | category | flops | bytes accessed | tf_op | source)
XLA Modules:
  0.0 99.6 jit_solution(4409141530607265167)
XLA Ops:
  1.3 0.0 copy-start.2
  1.3 0.0 copy-start.4
  1.3 6.7 %shard_map.85.whole = f32[3,512,512]{2,1,0:T(8,128)} custom-call(s32[1,4]{1,0:T(1,128)} %target.3, s32[1,1]{1,0:T(1,128)S(6)} %copy.12.count, f32[512,512]{1,0:T(8,128)} %bitcast.5, f32[1,4,512,512]{3,2,1,0:T(8,128)} %left_ref.3, f32[1,4,512,512]{3,2,1,0:T(8,128)} %right_ref.3), custom_call_target="tpu_custom_call" | custom-call | tf_op jit(solution)/shard_map/pallas_call | solution.py:53
  8.0 0.0 copy-done.2
  8.0 0.0 copy-done.4
  8.0 0.0 copy-start
  8.0 1.9 %copy-done = f32[3,512,512]{2,1,0:T(8,128)S(1)} copy-done((f32[3,512,512]{2,1,0:T(8,128)S(1)}, f32[3,512,512]{2,1,0:T(8,128)}, u32[]{:S(2)}) %copy-start) | copy-done | bytes 3145752
  9.9 49.8 %shard_map.86 = (f32[128,512]{1,0:T(8,128)S(1)}, f32[128,512]{1,0:T(8,128)S(1)}, f32[512,512]{1,0:T(8,128)S(1)}) custom-call(f32[3,512,512]{2,1,0:T(8,128)S(1)} %copy-done, f32[512,512]{1,0:T(8,128)S(1)} %bitcast.6, f32[128,512]{1,0:T(8,128)S(1)} %bitcast.8), custom_call_target="tpu_custom_call" | custom-call | tf_op jit(solution)/shard_map/pallas_call | solution.py:251
  59.7 0.0 copy-start.3
  59.7 1.0 copy-done.3
  60.7 6.6 %shard_map.87.whole = f32[3,512,512]{2,1,0:T(8,128)} custom-call(s32[1,4]{1,0:T(1,128)} %target.3, s32[1,1]{1,0:T(1,128)S(6)} %copy.12.count, f32[512,512]{1,0:T(8,128)} %copy-done.3, f32[1,4,512,512]{3,2,1,0:T(8,128)} %left_ref.3, f32[1,4,512,512]{3,2,1,0:T(8,128)} %right_ref.3), custom_call_target="tpu_custom_call" | custom-call | tf_op jit(solution)/shard_map/pallas_call | solution.py:53
  67.3 0.0 copy-start.1
  67.3 1.9 %copy-done.1 = f32[3,512,512]{2,1,0:T(8,128)S(1)} copy-done((f32[3,512,512]{2,1,0:T(8,128)S(1)}, f32[3,512,512]{2,1,0:T(8,128)}, u32[]{:S(2)}) %copy-start.1) | copy-done | bytes 3145752
  69.2 28.3 %shard_map.88 = f32[128,512]{1,0:T(8,128)S(1)} custom-call(f32[3,512,512]{2,1,0:T(8,128)S(1)} %copy-done.1), custom_call_target="tpu_custom_call" | custom-call | tf_op jit(solution)/shard_map/pallas_call | solution.py:265
  97.5 0.7 copy.13
  98.2 0.7 copy.14
  98.9 0.7 copy.15
Async XLA Ops:
  1.3 6.8 %copy-start.2 = (f32[1,512,512]{2,1,0:T(8,128)S(1)}, f32[1,512,512]{2,1,0:T(8,128)}, u32[]{:S(2)}) copy-start(f32[1,512,512]{2,1,0:T(8,128)} %param.6) | copy-start | bytes 3145732
  1.3 6.8 %copy-start.4 = (f32[1,128,512]{2,1,0:T(8,128)S(1)}, f32[1,128,512]{2,1,0:T(8,128)}, u32[]{:S(2)}) copy-start(f32[1,128,512]{2,1,0:T(8,128)} %param.7) | copy-start | bytes 786436
  8.0 1.9 %copy-start = (f32[3,512,512]{2,1,0:T(8,128)S(1)}, f32[3,512,512]{2,1,0:T(8,128)}, u32[]{:S(2)}) copy-start(f32[3,512,512]{2,1,0:T(8,128)} %shard_map.85.whole) | copy-start | bytes 9437188
  59.7 1.0 copy-start.3
  67.3 1.9 %copy-start.1 = (f32[3,512,512]{2,1,0:T(8,128)S(1)}, f32[3,512,512]{2,1,0:T(8,128)}, u32[]{:S(2)}) copy-start(f32[3,512,512]{2,1,0:T(8,128)} %shard_map.87.whole) | copy-start | bytes 9437188
